TPU v7x, 512 devices: a 4x2x32 block of a 4x8x32 slice. The times are simulated.
512 devices in a mesh: parts: 2 (over y), seq: 32 (over z), head: 8 (over x, core).
Axes of the slice: x: 4, y: 2, z: 32, core: 2. Of those that a mesh axis runs over, the one named last changes fastest.
The devices are a block of a 4x8x32 slice.
Arguments:
- hidden: bfloat16 [48, 12288], P(('parts', 'head'), 'seq'), parts along dimension 0, may hold values from -600 to 600
- norm_gain: float32 [12288], P('seq'), may hold values from 0.1 to 1.9
- w_query: bfloat16 [12288, 12288], P('seq', 'head'), may hold values from -0.0546875 to 0.0546875
- w_key: bfloat16 [12288, 1024], P('seq', 'head'), may hold values from -0.0546875 to 0.0546875
- w_value: bfloat16 [12288, 1024], P('seq', 'head'), may hold values from -0.0546875 to 0.0546875
- w_out: bfloat16 [12288, 12288], P('head', 'seq'), may hold values from -0.0546875 to 0.0546875
- lengths: int32 [48], P('parts'), parts along dimension 0, may hold values from 1 to 4096, as said below
- key_cache: bfloat16 [48, 8, 4096, 128], P('parts', 'head', 'seq'), parts along dimension 0, may hold values from -600 to 600, as said below
- value_cache: bfloat16 [48, 8, 4096, 128], P('parts', 'head', 'seq'), parts along dimension 0, may hold values from -6 to 6
Outputs:
- attn_out: bfloat16 [48, 12288], P(('parts', 'head'), 'seq'), parts along dimension 0
There are 2 independent parts, one for each index of `parts`. A program takes and returns all parts, laid end to end along the dimension named above; an argument that names none is the same for every part. Nothing has to cross between parts.
Inputs may be any that keep to these rules, and one draw needn't show every extreme that they name: Sequence b holds lengths[b] cached tokens at positions 0 to lengths[b] - 1; its new token takes position lengths[b]. `key_cache`: positions at or past a sequence's length hold no data.
All inputs are finite; a program needn't handle non-finite values.
Results may differ from a plain program's by a relative error of at most 0.0075.
The roundings to bfloat16 on the way count: a program that leaves them out, or rounds other values in their place, can miss the bound.
Values may be sent and summed in bfloat16 or wider, within the bound.
No kernel may reach another device: no remote copies, remote signals or barrier semaphores. Data moves between devices by JAX's collectives and lax.ppermute only.
A program may use at most 64 MiB of HBM per device.

v0:
```python
import math
import jax
import jax.numpy as jnp
from jax import lax
from jax.sharding import PartitionSpec as P

D = 12288
EPSILON = 1e-05


def in_order(tiles, dim):
    tiles = jnp.moveaxis(tiles, 0, dim)
    dims = tiles.shape
    return tiles.reshape(*dims[:dim], dims[dim] * dims[dim + 1], *dims[dim + 2 :])


def sent_to_all(x, axis):
    copies = jnp.broadcast_to(x, (lax.axis_size(axis), *x.shape))
    return lax.all_to_all(copies, axis, split_axis=0, concat_axis=0, tiled=True)


def gather_directly(x, axis, dim):
    return in_order(sent_to_all(x, axis), dim)


def cut_along(x, dim, peers):
    before, after = (x.shape[:dim], x.shape[dim + 1 :])
    return jnp.moveaxis(x.reshape(*before, peers, -1, *after), dim, 0)


def summed_on_arrival(x, axis, dim):
    tiles = cut_along(x, dim, lax.axis_size(axis))
    arrived = lax.all_to_all(tiles, axis, split_axis=0, concat_axis=0, tiled=True)
    return arrived.sum(axis=0)


def in_one_piece(arrays, axis, dim, along):
    ends, at = ([], 0)
    for a in arrays[:-1]:
        at += a.shape[along]
        ends.append(at)
    both = jnp.concatenate(arrays, axis=along)
    return tuple(jnp.split(summed_on_arrival(both, axis, dim), ends, axis=along))


def in_one_piece_2(arrays, axis, dim, along):
    ends, at = ([], 0)
    for a in arrays[:-1]:
        at += a.shape[along]
        ends.append(at)
    both = jnp.concatenate(arrays, axis=along)
    return tuple(jnp.split(lax.all_gather(both, axis, axis=dim, tiled=True), ends, axis=along))


def side_by_side(arrays, axis, dim, along):
    widths = [math.prod(a.shape[along:]) for a in arrays]
    both = jnp.concatenate(
        [a.reshape(*a.shape[:along], w) for a, w in zip(arrays, widths)], axis=along
    )
    result = lax.all_gather(both, axis, axis=dim, tiled=True)
    tiles = jnp.split(result, [sum(widths[:k]) for k in range(1, len(widths))], axis=along)
    return tuple(
        (b.reshape(*result.shape[:along], *a.shape[along:]) for a, b in zip(arrays, tiles))
    )


def fold_blocks(totals, pieces):
    new_max = jnp.maximum(totals[0], jnp.max(pieces[0], axis=0))
    piece_factor = jnp.exp(pieces[0] - new_max[None])
    den_total = jnp.sum(piece_factor * pieces[1], axis=0)
    acc_total = jnp.sum(piece_factor[..., None] * pieces[2], axis=0)
    return (new_max, den_total, acc_total)


def local(hidden, norm_gain, w_query, w_key, w_value, w_out, lengths, key_cache, value_cache):
    batch_size, kv_local, block_len, head_size = key_cache.shape
    group_size = w_query.shape[1] // (kv_local * head_size)
    token_rows = gather_directly(hidden, "head", 0)
    widened = token_rows.astype(jnp.float32)
    square_local = jnp.sum(widened * widened, axis=1)
    scaled = (widened * norm_gain).astype(jnp.bfloat16)
    query_part = jnp.dot(scaled, w_query, preferred_element_type=jnp.float32)
    key_part = jnp.dot(scaled, w_key, preferred_element_type=jnp.float32)
    value_part = jnp.dot(scaled, w_value, preferred_element_type=jnp.float32)
    query_factor = float(head_size) ** (-0.5)
    square_tiled = jnp.broadcast_to(square_local[:, None], (batch_size, lax.axis_size("seq")))
    query_sum, key_sum, value_sum, norm_column = (
        summed_on_arrival(query_part, "seq", 1),
        *in_one_piece((key_part, value_part), "seq", 1, 0),
        summed_on_arrival(square_tiled, "seq", 1),
    )
    norm_total = norm_column[:, 0]
    inverse_rms = lax.rsqrt(norm_total / D + EPSILON)[:, None]
    queries = (query_sum * inverse_rms * query_factor).astype(jnp.bfloat16)
    new_keys = (key_sum * inverse_rms).astype(jnp.bfloat16)
    new_values = (value_sum * inverse_rms).astype(jnp.bfloat16)
    queries, new_keys, new_values = (
        lax.all_gather(queries, "seq", axis=1, tiled=True),
        *in_one_piece_2((new_keys, new_values), "seq", 1, 0),
    )
    grouped = queries.reshape(batch_size, kv_local, group_size, head_size)
    scores = jnp.einsum("bkgd,bkpd->bkgp", grouped, key_cache, preferred_element_type=jnp.float32)
    offset = lax.axis_index("seq") * block_len
    positions = offset + jnp.arange(block_len, dtype=jnp.int32)
    live_mask = (positions[None, :] < lengths[:, None])[:, None, None, :]
    block_max = jnp.max(jnp.where(live_mask, scores, -1e30), axis=-1)
    shifted = jnp.where(live_mask, scores - block_max[..., None], 0.0)
    weights = jnp.where(live_mask, jnp.exp(shifted), 0.0).astype(jnp.bfloat16)
    block_den = jnp.sum(weights.astype(jnp.float32), axis=-1)
    block_acc = jnp.einsum(
        "bkgp,bkpd->bkgd", weights, value_cache, preferred_element_type=jnp.float32
    )
    self_score = jnp.einsum(
        "oips,ois->oip",
        grouped,
        new_keys.reshape(batch_size, kv_local, head_size),
        preferred_element_type=jnp.float32,
    )
    initial = (
        jnp.full(block_max.shape, -1e30, jnp.float32),
        jnp.zeros(block_den.shape, jnp.float32),
        jnp.zeros(block_acc.shape, jnp.float32),
    )
    global_max, den_merged, acc_merged = fold_blocks(
        initial, side_by_side((block_max[None], block_den[None], block_acc[None]), "seq", 0, 4)
    )
    top_score = jnp.maximum(global_max, self_score)
    factors = jnp.exp(global_max - top_score)
    den_sum = den_merged * factors
    acc_sum = acc_merged * factors[..., None]
    own_weight = jnp.exp(self_score - top_score)
    denominator = den_sum + own_weight
    numerator = acc_sum + own_weight[..., None] * new_values.reshape(
        batch_size, kv_local, 1, head_size
    ).astype(jnp.float32)
    mixed = (
        (numerator / denominator[..., None])
        .astype(jnp.bfloat16)
        .reshape(batch_size, kv_local * group_size * head_size)
    )
    output = summed_on_arrival(jnp.dot(mixed, w_out, preferred_element_type=jnp.float32), "head", 0)
    return output.astype(jnp.bfloat16)


def solution(mesh):
    return jax.shard_map(
        local,
        mesh=mesh,
        in_specs=(
            P(("parts", "head"), "seq"),
            P("seq"),
            P("seq", "head"),
            P("seq", "head"),
            P("seq", "head"),
            P("head", "seq"),
            P("parts"),
            P("parts", "head", "seq", None),
            P("parts", "head", "seq", None),
        ),
        out_specs=P(("parts", "head"), "seq"),
        check_vma=False,
    )
```

profile of v0, /device:TPU:33, one launch (start us, length us, event | category | flops | bytes accessed | tf_op | source)
XLA Modules:
  0.0 357.4 jit_solution(9531133762320092091)
XLA Ops:
  6.5 0.0 copy-start
  6.6 0.0 copy-start.1
  6.6 1.4 broadcast_in_dim.49
  8.0 44.7 %all-to-all-start = ((bf16[8,3,384]{2,1,0:T(4,128)(2,1)}), bf16[8,3,384]{2,1,0:T(4,128)(2,1)S(1)}, u32[]{:S(2)}, u32[]{:S(2)}) async-start(bf16[8,3,384]{2,1,0:T(4,128)(2,1)} %broadcast_in_dim.49), calls=%async_computation | async-start | bytes 49152 | tf_op jit(solution)/shard_map/all_to_all | solution.py:19
  52.7 1.7 copy.66
  54.4 3.0 all-to-all-done
  57.4 0.8 multiply_reduce_fusion
  58.2 0.1 broadcast_in_dim.50
  58.3 0.6 transpose.24
  58.9 6.8 %all-to-all-start.2 = ((f32[32,24,1]{1,2,0:T(1,128)}), f32[32,24,1]{1,2,0:T(1,128)S(1)}, u32[]{:S(2)}, u32[]{:S(2)}) async-start(f32[32,24,1]{1,2,0:T(1,128)} %transpose.24), calls=%async_computation.2 | async-start | bytes 32768 | tf_op jit(solution)/shard_map/all_to_all | solution.py:33
  65.7 0.6 reshape.201
  66.3 0.0 copy-done.3
  66.3 1.6 convolution_bitcast_fusion
  67.8 1.1 reshape.206
  68.9 17.3 %all-to-all-done.2 = f32[32,24,1]{1,2,0:T(1,128)S(1)} async-done(((f32[32,24,1]{1,2,0:T(1,128)}), f32[32,24,1]{1,2,0:T(1,128)S(1)}, u32[]{:S(2)}, u32[]{:S(2)}) %all-to-all-start.2) | async-done | bytes 3104 | tf_op jit(solution)/shard_map/all_to_all | solution.py:33
  86.2 4.8 %all-to-all-start.1 = ((f32[32,1,1152]{2,1,0:T(1,128)}), f32[32,1,1152]{2,1,0:T(1,128)S(1)}, u32[]{:S(2)}, u32[]{:S(2)}) async-start(f32[32,1,1152]{2,1,0:T(1,128)} %reshape.206), calls=%async_computation.1 | async-start | bytes 294912 | tf_op jit(solution)/shard_map/all_to_all | solution.py:33
  91.0 0.1 all-gather.4.cloned.1.call-start
  91.1 0.7 broadcast_compare_fusion
  91.8 0.1 reduce_sum.74
  91.9 27.9 %all-to-all-done.1 = f32[32,1,1152]{2,1,0:T(1,128)S(1)} async-done(((f32[32,1,1152]{2,1,0:T(1,128)}), f32[32,1,1152]{2,1,0:T(1,128)S(1)}, u32[]{:S(2)}, u32[]{:S(2)}) %all-to-all-start.1) | async-done | bytes 147488 | tf_op jit(solution)/shard_map/all_to_all | solution.py:33
  119.8 0.5 broadcast.93
  120.3 1.0 reduce.10
  121.3 0.2 reshape.207
  121.6 0.1 fusion.13
  121.7 38.6 %all-gather = bf16[32,48,24]{1,2,0:T(8,128)(2,1)S(1)} all-gather(bf16[1,48,24]{1,2,0:T(8,128)(2,1)S(1)} %fusion.13), channel_id=1, replica_groups=mesh['parts'=2,'seq'=32,'head'=8] {'seq'}, dimensions={0}, use_global_device_ids=true | all-gather | bytes 76032 | tf_op jit(solution)/shard_map/all_gather | solution.py:98
  160.3 0.3 reshape.198
  160.5 0.1 reshape.190
  160.6 0.0 copy-done.1
  160.6 0.6 select_reduce_fusion
  161.2 0.2 convert_reduce_fusion
  161.5 0.0 copy-done.2
  161.5 0.4 convolution_bitcast_fusion.1
  161.9 0.3 copy.71
  162.1 0.3 copy.70
  162.4 0.3 pad_maximum_fusion
  162.7 0.9 copy.72
  163.6 0.1 all-gather.4.cloned.1.call-update
  163.6 0.0 copy-done.4
  163.6 1.0 fusion.14
  164.7 1.0 fusion.15
  165.8 0.1 copy.75
  165.9 0.1 reshape.208
  166.0 30.1 %all_to_all.25 = f32[32,1,192]{2,1,0:T(1,128)S(1)} all-to-all(f32[32,1,192]{2,1,0:T(1,128)S(1)} %reshape.208), channel_id=1, replica_groups=mesh['parts'=2,'seq'=32,'head'=8] {'seq'}, dimensions={0} | all-to-all | bytes 49152 | tf_op jit(solution)/shard_map/all_to_all | solution.py:33
  196.1 0.7 reduce.11
  196.8 0.1 reshape.209
  197.0 0.1 multiply_convert_fusion.6
  197.1 0.1 maximum_bitcast_fusion
  197.1 42.9 %all-gather.1 = bf16[32,4,48]{2,1,0:T(4,128)(2,1)S(1)} all-gather(bf16[1,4,48]{2,1,0:T(4,128)(2,1)S(1)} %maximum_bitcast_fusion), channel_id=1, replica_groups=mesh['parts'=2,'seq'=32,'head'=8] {'seq'}, dimensions={0}, use_global_device_ids=true | all-gather | bytes 12672 | tf_op jit(solution)/shard_map/all_gather | solution.py:52
  240.0 0.1 copy.76
  240.1 0.2 fusion.9
  240.3 0.1 copy.82
  240.4 61.3 %all-gather.4.cloned.1.call-done = f32[32,24,1,12,130]{4,1,3,2,0:T(8,128)} async-done(((f32[1,24,1,12,130]{4,1,3,2,0:T(8,128)}), f32[32,24,1,12,130]{4,1,3,2,0:T(8,128)}) %all-gather.4.cloned.1.call-update) | async-done | bytes 4792336 | tf_op jit(solution)/shard_map/all_gather | solution.py:60
  301.7 9.1 %fusion.18 = (f32[32,24,1,12,1]{4,1,3,2,0:T(8,128)}, f32[24,12]{0,1:T(8,128)S(1)}, f32[32,24,1,12,1]{4,1,3,2,0:T(8,128)}) fusion(f32[32,24,1,12,130]{4,1,3,2,0:T(8,128)} %all-gather.4.cloned.1.call-done), kind=kLoop, calls=%fused_computation.45 | loop fusion | flops 8928 | bytes 148608 | tf_op jit(solution)/shard_map/split | solution.py:61
  310.8 3.5 copy.88
  314.3 3.5 copy.87
  317.9 0.1 exponential_bitcast_fusion
  318.0 0.2 fusion.6
  318.2 0.2 copy.74
  318.4 5.1 %fusion = f32[24,12,128]{2,0,1:T(8,128)S(1)} fusion(f32[32,24,1,12,130]{4,1,3,2,0:T(8,128)} %all-gather.4.cloned.1.call-done, f32[32,24,12]{1,2,0:T(8,128)S(1)} %copy.74), kind=kLoop, calls=%fused_computation.1 | loop fusion | flops 2322432 | bytes 4902912 | tf_op jit(solution)/shard_map/reduce_sum | solution.py:71
  323.5 0.2 divide_convert_fusion
  323.7 0.0 copy-done
  323.7 0.3 fusion.1
  324.0 25.8 %all_to_all.26 = f32[8,3,384]{2,1,0:T(4,128)S(1)} all-to-all(f32[8,3,384]{2,1,0:T(4,128)S(1)} %copy.80), channel_id=1, replica_groups=mesh['parts'=2,'seq'=32,'head'=8] {'head'}, dimensions={0} | all-to-all | bytes 73728 | tf_op jit(solution)/shard_map/all_to_all | solution.py:33
  349.9 0.6 reduce_sum.79
  (16 shorter events, 0.3 us)
Async XLA Ops:
  6.5 317.2 %copy-start = (bf16[1536,384]{1,0:T(8,128)(2,1)S(1)}, bf16[1536,384]{1,0:T(8,128)(2,1)}, u32[]{:S(2)}) copy-start(bf16[1536,384]{1,0:T(8,128)(2,1)} %param.14) | copy-start | bytes 3538948
  6.6 154.1 %copy-start.1 = (bf16[24,1,128,128]{3,2,1,0:T(8,128)(2,1)S(1)}, bf16[24,1,128,128]{3,2,1,0:T(8,128)(2,1)}, u32[]{:S(2)}) copy-start(bf16[24,1,128,128]{3,2,1,0:T(8,128)(2,1)} %param.16) | copy-start | bytes 2359300
  8.0 49.4 %all-to-all-start = ((bf16[8,3,384]{2,1,0:T(4,128)(2,1)}), bf16[8,3,384]{2,1,0:T(4,128)(2,1)S(1)}, u32[]{:S(2)}, u32[]{:S(2)}) async-start(bf16[8,3,384]{2,1,0:T(4,128)(2,1)} %broadcast_in_dim.49), calls=%async_computation | async-start | bytes 49152 | tf_op jit(solution)/shard_map/all_to_all | solution.py:19
  57.4 8.9 %copy-start.3 = (bf16[8,3,384]{2,1,0:T(4,128)(2,1)}, bf16[8,3,384]{2,1,0:T(4,128)(2,1)S(1)}, u32[]{:S(2)}) copy-start(bf16[8,3,384]{2,1,0:T(4,128)(2,1)S(1)} %all-to-all-done) | copy-start | bytes 55300
  58.9 27.3 %all-to-all-start.2 = ((f32[32,24,1]{1,2,0:T(1,128)}), f32[32,24,1]{1,2,0:T(1,128)S(1)}, u32[]{:S(2)}, u32[]{:S(2)}) async-start(f32[32,24,1]{1,2,0:T(1,128)} %transpose.24), calls=%async_computation.2 | async-start | bytes 32768 | tf_op jit(solution)/shard_map/all_to_all | solution.py:33
  67.8 93.6 %copy-start.2 = (bf16[24,1,128,128]{3,2,1,0:T(8,128)(2,1)S(1)}, bf16[24,1,128,128]{3,2,1,0:T(8,128)(2,1)}, u32[]{:S(2)}) copy-start(bf16[24,1,128,128]{3,2,1,0:T(8,128)(2,1)} %param.17) | copy-start | bytes 2359300
  68.9 94.7 %copy-start.4 = (bf16[8,3,384]{2,1,0:T(4,128)(2,1)S(1)}, bf16[8,3,384]{2,1,0:T(4,128)(2,1)}, u32[]{:S(2)}) copy-start(bf16[8,3,384]{2,1,0:T(4,128)(2,1)} %copy-done.3) | copy-start | bytes 55300
  86.2 33.6 %all-to-all-start.1 = ((f32[32,1,1152]{2,1,0:T(1,128)}), f32[32,1,1152]{2,1,0:T(1,128)S(1)}, u32[]{:S(2)}, u32[]{:S(2)}) async-start(f32[32,1,1152]{2,1,0:T(1,128)} %reshape.206), calls=%async_computation.1 | async-start | bytes 294912 | tf_op jit(solution)/shard_map/all_to_all | solution.py:33
  91.0 210.7 %all-gather.4.cloned.1.call-start = ((), (), s32[]{:S(2)}) async-start(), calls=%async_computation.5 | async-start | bytes 9732096 | tf_op jit(solution)/shard_map/all_gather | solution.py:60
Sparse Core Ops, SparseCore 0:
  163.7 137.9 all-gather.3
where the time goes:
time: 358 us; the launch traced here: 357 us
  blocking collectives  137 us (38%)
  waiting for transfers between devices  110 us (31%)
  starting transfers between devices  56.3 us (16%)
  other arithmetic  19.4 us (5%)
  local copies, waits for them, and re-layouts  15.8 us (4%)
  between operations  13.7 us (4%)
  matrix products  5.05 us (1%)
    all_gather x1, waiting for transfers between devices, side_by_side(): result = lax.all_gather(both, axis, axis=dim, tiled=True)  61.3 us
    all_to_all x2, blocking collectives, summed_on_arrival(): lax.all_to_all(tiles, axis, split_axis=0, concat_axis=0, tiled=True)  56 us
    all_to_all x2, waiting for transfers between devices, summed_on_arrival(): lax.all_to_all(tiles, axis, split_axis=0, concat_axis=0, tiled=True)  45.3 us
    all_to_all x1, starting transfers between devices, sent_to_all(): return lax.all_to_all(copies, axis, split_axis=0, concat_axis=0, tiled=True)  44.7 us
    all_gather x1, blocking collectives, in_one_piece_2(): lax.all_gather(both, axis, axis=dim, tiled=True)  42.9 us
    all_gather x1, blocking collectives, local(): lax.all_gather(queries, 'seq', axis=1, tiled=True)  38.6 us
    all_to_all x2, starting transfers between devices, summed_on_arrival(): lax.all_to_all(tiles, axis, split_axis=0, concat_axis=0, tiled=True)  11.5 us
    unnamed x19, local copies, waits for them, and re-layouts  10.6 us
  transfers between devices with their start and end apart: 4, of which 4 were waited for; matrix products, arithmetic and copies ran while one was open for 3% of the time, Pallas kernels for 0%

commit v1 on v0

--- a/solution.py
+++ b/solution.py
@@ -95,7 +95,9 @@
     new_keys = (key_sum * inverse_rms).astype(jnp.bfloat16)
     new_values = (value_sum * inverse_rms).astype(jnp.bfloat16)
     queries, new_keys, new_values = (
-        lax.all_gather(queries, "seq", axis=1, tiled=True),
+        jnp.concatenate(
+            lax.all_to_all(jnp.stack([queries] * lax.axis_size("seq")), "seq", 0, 0), axis=1
+        ),
         *in_one_piece_2((new_keys, new_values), "seq", 1, 0),
     )
     grouped = queries.reshape(batch_size, kv_local, group_size, head_size)

time: 358 us -> 332 us (0.927)
  blocking collectives: 137 us -> 92.8 us
  waiting for transfers between devices: 110 us -> 122 us
  starting transfers between devices: 56.3 us -> 62.1 us
    all_gather x1 -> x0, blocking collectives: 38.6 us -> none  [local(): lax.all_gather(queries, 'seq', axis=1, tiled=True)]
    all_to_all x0 -> x1, waiting for transfers between devices: none -> 22.5 us  [local(): lax.all_to_all(jnp.stack([queries] * lax.axis_size('seq')), 'seq', 0, 0)]
    all_gather x1, waiting for transfers between devices: 61.3 us -> 50.7 us  [side_by_side(): result = lax.all_gather(both, axis, axis=dim, tiled=True)]
    all_to_all x0 -> x1, starting transfers between devices: none -> 5.86 us  [local(): lax.all_to_all(jnp.stack([queries] * lax.axis_size('seq')), 'seq', 0, 0)]
    all_to_all x2, blocking collectives: 56 us -> 50.5 us  [summed_on_arrival(): lax.all_to_all(tiles, axis, split_axis=0, concat_axis=0, tiled=True)]
    unnamed x19 -> x24, local copies, waits for them, and re-layouts: 10.6 us -> 11.4 us
  transfers between devices with their start and end apart: 4 -> 5, of which waited for: 4 -> 5; matrix products, arithmetic and copies ran while one was open for 3% -> 3% of each run, Pallas kernels for 0% -> 0%
where the time goes in v1:
time: 332 us; the launch traced here: 331 us
  waiting for transfers between devices  122 us (37%)
  blocking collectives  92.8 us (28%)
  starting transfers between devices  62.1 us (19%)
  other arithmetic  19.4 us (6%)
  local copies, waits for them, and re-layouts  16.8 us (5%)
  between operations  13.7 us (4%)
  matrix products  4.13 us (1%)
    all_gather x1, waiting for transfers between devices, side_by_side(): result = lax.all_gather(both, axis, axis=dim, tiled=True)  50.7 us
    all_to_all x2, blocking collectives, summed_on_arrival(): lax.all_to_all(tiles, axis, split_axis=0, concat_axis=0, tiled=True)  50.5 us
    all_to_all x2, waiting for transfers between devices, summed_on_arrival(): lax.all_to_all(tiles, axis, split_axis=0, concat_axis=0, tiled=True)  46.1 us
    all_to_all x1, starting transfers between devices, sent_to_all(): return lax.all_to_all(copies, axis, split_axis=0, concat_axis=0, tiled=True)  44.7 us
    all_gather x1, blocking collectives, in_one_piece_2(): lax.all_gather(both, axis, axis=dim, tiled=True)  42.3 us
    all_to_all x1, waiting for transfers between devices, local(): lax.all_to_all(jnp.stack([queries] * lax.axis_size('seq')), 'seq', 0, 0)  22.5 us
    all_to_all x2, starting transfers between devices, summed_on_arrival(): lax.all_to_all(tiles, axis, split_axis=0, concat_axis=0, tiled=True)  11.5 us
    unnamed x24, local copies, waits for them, and re-layouts  11.4 us
  transfers between devices with their start and end apart: 5, of which 5 were waited for; matrix products, arithmetic and copies ran while one was open for 3% of the time, Pallas kernels for 0%

profile of v1, /device:TPU:33, one launch (start us, length us, event | category | flops | bytes accessed | tf_op | source)
XLA Modules:
  0.0 331.3 jit_solution(8045730332291931779)
XLA Ops:
  6.5 0.0 copy-start
  6.6 1.4 broadcast_in_dim.49
  8.0 44.7 %all-to-all-start = ((bf16[8,3,384]{2,1,0:T(4,128)(2,1)}), bf16[8,3,384]{2,1,0:T(4,128)(2,1)S(1)}, u32[]{:S(2)}, u32[]{:S(2)}) async-start(bf16[8,3,384]{2,1,0:T(4,128)(2,1)} %broadcast_in_dim.49), calls=%async_computation | async-start | bytes 49152 | tf_op jit(solution)/shard_map/all_to_all | solution.py:19
  52.7 1.7 copy.65
  54.4 3.0 all-to-all-done
  57.4 0.8 multiply_reduce_fusion
  58.2 0.1 broadcast_in_dim.50
  58.3 0.6 transpose.24
  58.9 6.8 %all-to-all-start.2 = ((f32[32,24,1]{1,2,0:T(1,128)}), f32[32,24,1]{1,2,0:T(1,128)S(1)}, u32[]{:S(2)}, u32[]{:S(2)}) async-start(f32[32,24,1]{1,2,0:T(1,128)} %transpose.24), calls=%async_computation.2 | async-start | bytes 32768 | tf_op jit(solution)/shard_map/all_to_all | solution.py:33
  65.7 0.6 reshape.210
  66.3 0.0 copy-done.3
  66.3 1.6 convolution_bitcast_fusion
  67.8 1.1 reshape.215
  68.9 17.3 %all-to-all-done.2 = f32[32,24,1]{1,2,0:T(1,128)S(1)} async-done(((f32[32,24,1]{1,2,0:T(1,128)}), f32[32,24,1]{1,2,0:T(1,128)S(1)}, u32[]{:S(2)}, u32[]{:S(2)}) %all-to-all-start.2) | async-done | bytes 3104 | tf_op jit(solution)/shard_map/all_to_all | solution.py:33
  86.2 4.8 %all-to-all-start.1 = ((f32[32,1,1152]{2,1,0:T(1,128)}), f32[32,1,1152]{2,1,0:T(1,128)S(1)}, u32[]{:S(2)}, u32[]{:S(2)}) async-start(f32[32,1,1152]{2,1,0:T(1,128)} %reshape.215), calls=%async_computation.1 | async-start | bytes 294912 | tf_op jit(solution)/shard_map/all_to_all | solution.py:33
  91.0 0.1 reduce_sum.74
  91.1 28.7 %all-to-all-done.1 = f32[32,1,1152]{2,1,0:T(1,128)S(1)} async-done(((f32[32,1,1152]{2,1,0:T(1,128)}), f32[32,1,1152]{2,1,0:T(1,128)S(1)}, u32[]{:S(2)}, u32[]{:S(2)}) %all-to-all-start.1) | async-done | bytes 147488 | tf_op jit(solution)/shard_map/all_to_all | solution.py:33
  119.8 0.5 broadcast.98
  120.3 1.0 reduce.10
  121.3 0.2 reshape.216
  121.6 0.1 multiply_convert_fusion.2
  121.7 0.9 reshape.217
  122.6 5.9 %all-to-all-start.3 = ((bf16[32,2,576]{2,1,0:T(2,128)(2,1)}), bf16[32,2,576]{2,1,0:T(2,128)(2,1)S(1)}, u32[]{:S(2)}, u32[]{:S(2)}) async-start(bf16[32,2,576]{2,1,0:T(2,128)(2,1)} %reshape.217), calls=%async_computation.3 | async-start | bytes 163840 | tf_op jit(solution)/shard_map/all_to_all | solution.py:99
  128.5 0.1 all-gather.3.cloned.1.call-start
  128.6 0.7 broadcast_compare_fusion
  129.3 22.5 %all-to-all-done.3 = bf16[32,2,576]{2,1,0:T(2,128)(2,1)S(1)} async-done(((bf16[32,2,576]{2,1,0:T(2,128)(2,1)}), bf16[32,2,576]{2,1,0:T(2,128)(2,1)S(1)}, u32[]{:S(2)}, u32[]{:S(2)}) %all-to-all-start.3) | async-done | bytes 73760 | tf_op jit(solution)/shard_map/all_to_all | solution.py:99
  151.8 0.2 reshape.218
  152.1 0.2 reshape.201
  152.3 0.0 copy-done.1
  152.3 0.6 select_reduce_fusion
  152.9 0.2 convert_reduce_fusion
  153.1 0.4 convolution_bitcast_fusion.1
  153.5 0.3 copy.70
  153.8 0.3 copy.69
  154.0 0.3 pad_maximum_fusion
  154.3 0.9 copy.71
  155.2 0.1 all-gather.3.cloned.1.call-update
  155.3 0.0 copy-done.4
  155.3 0.1 fusion.13
  155.5 1.0 fusion.14
  156.5 0.1 copy.74
  156.6 0.1 reshape.219
  156.7 25.1 %all_to_all.30 = f32[32,1,192]{2,1,0:T(1,128)S(1)} all-to-all(f32[32,1,192]{2,1,0:T(1,128)S(1)} %reshape.219), channel_id=1, replica_groups=mesh['parts'=2,'seq'=32,'head'=8] {'seq'}, dimensions={0} | all-to-all | bytes 49152 | tf_op jit(solution)/shard_map/all_to_all | solution.py:33
  181.8 0.7 reduce.11
  182.5 0.1 reshape.220
  182.7 0.1 multiply_convert_fusion.6
  182.8 0.1 maximum_bitcast_fusion
  182.8 42.3 %all-gather = bf16[32,4,48]{2,1,0:T(4,128)(2,1)S(1)} all-gather(bf16[1,4,48]{2,1,0:T(4,128)(2,1)S(1)} %maximum_bitcast_fusion), channel_id=1, replica_groups=mesh['parts'=2,'seq'=32,'head'=8] {'seq'}, dimensions={0}, use_global_device_ids=true | all-gather | bytes 12672 | tf_op jit(solution)/shard_map/all_gather | solution.py:52
  225.1 0.1 copy.75
  225.2 0.2 fusion.9
  225.4 0.1 copy.81
  225.5 50.7 %all-gather.3.cloned.1.call-done = f32[32,24,1,12,130]{4,1,3,2,0:T(8,128)} async-done(((f32[1,24,1,12,130]{4,1,3,2,0:T(8,128)}), f32[32,24,1,12,130]{4,1,3,2,0:T(8,128)}) %all-gather.3.cloned.1.call-update) | async-done | bytes 4792336 | tf_op jit(solution)/shard_map/all_gather | solution.py:60
  276.1 9.1 %fusion.17 = (f32[32,24,1,12,1]{4,1,3,2,0:T(8,128)}, f32[24,12]{0,1:T(8,128)S(1)}, f32[32,24,1,12,1]{4,1,3,2,0:T(8,128)}) fusion(f32[32,24,1,12,130]{4,1,3,2,0:T(8,128)} %all-gather.3.cloned.1.call-done), kind=kLoop, calls=%fused_computation.44 | loop fusion | flops 8928 | bytes 148608 | tf_op jit(solution)/shard_map/split | solution.py:61
  285.2 3.5 %copy.87 = f32[32,24,1,12,1]{0,1,4,3,2:T(8,128)S(1)} copy(f32[32,24,1,12,1]{4,1,3,2,0:T(8,128)} %get-tuple-element.8) | data formatting | bytes 73728
  288.7 3.5 %copy.86 = f32[32,24,1,12,1]{0,1,4,3,2:T(8,128)S(1)} copy(f32[32,24,1,12,1]{4,1,3,2,0:T(8,128)} %get-tuple-element.10) | data formatting | bytes 73728
  292.3 0.1 exponential_bitcast_fusion
  292.4 0.2 fusion.6
  292.6 0.2 copy.73
  292.8 5.1 %fusion = f32[24,12,128]{2,0,1:T(8,128)S(1)} fusion(f32[32,24,1,12,130]{4,1,3,2,0:T(8,128)} %all-gather.3.cloned.1.call-done, f32[32,24,12]{1,2,0:T(8,128)S(1)} %copy.73), kind=kLoop, calls=%fused_computation.1 | loop fusion | flops 2322432 | bytes 4902912 | tf_op jit(solution)/shard_map/reduce_sum | solution.py:71
  297.9 0.2 divide_convert_fusion
  298.1 0.0 copy-done
  298.1 0.3 fusion.1
  298.4 25.4 %all_to_all.31 = f32[8,3,384]{2,1,0:T(4,128)S(1)} all-to-all(f32[8,3,384]{2,1,0:T(4,128)S(1)} %copy.79), channel_id=1, replica_groups=mesh['parts'=2,'seq'=32,'head'=8] {'head'}, dimensions={0} | all-to-all | bytes 73728 | tf_op jit(solution)/shard_map/all_to_all | solution.py:33
  323.9 0.6 reduce_sum.79
  (23 shorter events, 0.3 us)
Async XLA Ops:
  6.5 291.6 %copy-start = (bf16[1536,384]{1,0:T(8,128)(2,1)S(1)}, bf16[1536,384]{1,0:T(8,128)(2,1)}, u32[]{:S(2)}) copy-start(bf16[1536,384]{1,0:T(8,128)(2,1)} %param.14) | copy-start | bytes 3538948
  6.6 145.7 %copy-start.1 = (bf16[24,1,128,128]{3,2,1,0:T(8,128)(2,1)S(1)}, bf16[24,1,128,128]{3,2,1,0:T(8,128)(2,1)}, u32[]{:S(2)}) copy-start(bf16[24,1,128,128]{3,2,1,0:T(8,128)(2,1)} %param.16) | copy-start | bytes 2359300
  8.0 49.4 %all-to-all-start = ((bf16[8,3,384]{2,1,0:T(4,128)(2,1)}), bf16[8,3,384]{2,1,0:T(4,128)(2,1)S(1)}, u32[]{:S(2)}, u32[]{:S(2)}) async-start(bf16[8,3,384]{2,1,0:T(4,128)(2,1)} %broadcast_in_dim.49), calls=%async_computation | async-start | bytes 49152 | tf_op jit(solution)/shard_map/all_to_all | solution.py:19
  57.4 8.9 %copy-start.3 = (bf16[8,3,384]{2,1,0:T(4,128)(2,1)}, bf16[8,3,384]{2,1,0:T(4,128)(2,1)S(1)}, u32[]{:S(2)}) copy-start(bf16[8,3,384]{2,1,0:T(4,128)(2,1)S(1)} %all-to-all-done) | copy-start | bytes 55300
  58.9 27.3 %all-to-all-start.2 = ((f32[32,24,1]{1,2,0:T(1,128)}), f32[32,24,1]{1,2,0:T(1,128)S(1)}, u32[]{:S(2)}, u32[]{:S(2)}) async-start(f32[32,24,1]{1,2,0:T(1,128)} %transpose.24), calls=%async_computation.2 | async-start | bytes 32768 | tf_op jit(solution)/shard_map/all_to_all | solution.py:33
  67.8 85.3 %copy-start.2 = (bf16[24,1,128,128]{3,2,1,0:T(8,128)(2,1)S(1)}, bf16[24,1,128,128]{3,2,1,0:T(8,128)(2,1)}, u32[]{:S(2)}) copy-start(bf16[24,1,128,128]{3,2,1,0:T(8,128)(2,1)} %param.17) | copy-start | bytes 2359300
  68.9 86.4 %copy-start.4 = (bf16[8,3,384]{2,1,0:T(4,128)(2,1)S(1)}, bf16[8,3,384]{2,1,0:T(4,128)(2,1)}, u32[]{:S(2)}) copy-start(bf16[8,3,384]{2,1,0:T(4,128)(2,1)} %copy-done.3) | copy-start | bytes 55300
  68.9 86.4 %copy-start.5 = (bf16[384,128]{1,0:T(8,128)(2,1)S(1)}, bf16[384,128]{1,0:T(8,128)(2,1)}, u32[]{:S(2)}) copy-start(bf16[384,128]{1,0:T(8,128)(2,1)} %param.13) | copy-start | bytes 294916
  68.9 86.4 %copy-start.6 = (f32[384]{0:T(512)S(1)}, f32[384]{0:T(512)}, u32[]{:S(2)}) copy-start(f32[384]{0:T(512)} %param.10) | copy-start | bytes 4612
  86.2 33.6 %all-to-all-start.1 = ((f32[32,1,1152]{2,1,0:T(1,128)}), f32[32,1,1152]{2,1,0:T(1,128)S(1)}, u32[]{:S(2)}, u32[]{:S(2)}) async-start(f32[32,1,1152]{2,1,0:T(1,128)} %reshape.215), calls=%async_computation.1 | async-start | bytes 294912 | tf_op jit(solution)/shard_map/all_to_all | solution.py:33
  122.6 29.2 %all-to-all-start.3 = ((bf16[32,2,576]{2,1,0:T(2,128)(2,1)}), bf16[32,2,576]{2,1,0:T(2,128)(2,1)S(1)}, u32[]{:S(2)}, u32[]{:S(2)}) async-start(bf16[32,2,576]{2,1,0:T(2,128)(2,1)} %reshape.217), calls=%async_computation.3 | async-start | bytes 163840 | tf_op jit(solution)/shard_map/all_to_all | solution.py:99
  128.5 147.6 %all-gather.3.cloned.1.call-start = ((), (), s32[]{:S(2)}) async-start(), calls=%async_computation.6 | async-start | bytes 9732096 | tf_op jit(solution)/shard_map/all_gather | solution.py:60
Sparse Core Ops, SparseCore 0:
  155.4 120.6 all-gather.2
